TPU v7x, 32 devices: a whole 2x2x4 slice. The times are simulated.
32 devices in a mesh: path: 8 (over z, core), tm: 4 (over y, x).
Axes of the slice: x: 2, y: 2, z: 4, core: 2. Of those that a mesh axis runs over, the one named last changes fastest.
Arguments:
- shock_rate: float32 [64, 131072], P('tm', 'path'), may hold values from -6 to 6
- shock_fx: float32 [4, 64, 131072], P(None, 'tm', 'path'), may hold values from -6 to 6
- fx_vol: float32 [4], replicated, may hold values from 0.1 to 0.4
- fx_corr: float32 [4], replicated, may hold values from -0.8 to 0.8
- hazard_scale: float32 [32], replicated, may hold values from 0.03 to 3
- counterparty: int32 [512], replicated, may hold values from 0 to 31
- currency: int32 [512], replicated, may hold values from 0 to 3
- maturity: int32 [512], replicated, may hold values from 1 to 64
- notional: float32 [512], replicated, may hold values from -8 to 8
- strike: float32 [512], replicated, may hold values from 0.7 to 1.3
Outputs:
- profile: float32 [64, 32], P('tm')
- cva: float32 [32], replicated
All inputs are finite; a program needn't handle non-finite values.
Results may differ from a plain program's by a relative error of at most 0.000061.
Values sent between devices are 32-bit elements; how exact they have to be, the bound alone decides.
A program may use at most 64 MiB of HBM per device.

v0:
```python
import math

import jax
import jax.numpy as jnp
from jax import lax
from jax.sharding import PartitionSpec as P

HORIZON = 5.0
RATE_DOM = 0.03
RATE_FOR = 0.01
LOSS_SHARE = 0.6
RATE_SHIFT = 1.5
HIGHEST_PREC = lax.Precision.HIGHEST


def carried_in(part, axis, combine, identity):
    place = lax.axis_index(axis)
    gathered = jax.tree.map(lambda a: lax.all_gather(a, axis), part)
    state = jax.tree.map(lambda a, e: jnp.zeros_like(a) + jnp.asarray(e, a.dtype), part, identity)

    def one(turn, state):
        return combine(
            state, jax.tree.map(lambda a: lax.dynamic_index_in_dim(a, turn, 0, False), gathered)
        )

    return lax.fori_loop(0, place, one, state)


def trade_tables(
    date_rows, counterparty, currency, maturity, notional, strike, cp_count, ccy_count, date_step
):
    is_alive = (date_rows[:, None] < maturity[None, :]).astype(jnp.float32)
    time_left = (maturity[None, :] - date_rows[:, None]).astype(jnp.float32) * date_step
    weight_for = is_alive * notional[None, :] * jnp.exp(-RATE_FOR * time_left)
    weight_dom = is_alive * (notional * strike)[None, :] * jnp.exp(-RATE_DOM * time_left)
    member = (counterparty[None, :] == jnp.arange(cp_count, dtype=jnp.int32)[:, None]).astype(
        jnp.float32
    )
    currency_onehot = (currency[None, :] == jnp.arange(ccy_count, dtype=jnp.int32)[:, None]).astype(
        jnp.float32
    )
    fwd_table = jnp.einsum(
        "ck,tk,jk->tcj", member, weight_for, currency_onehot, precision=HIGHEST_PREC
    )
    dom_table = jnp.einsum("ck,tk->tc", member, weight_dom, precision=HIGHEST_PREC)
    return (fwd_table, dom_table)


def weigh_block(block_item, hazard_scale):
    fwd_table, dom_table, spot, hazard_prev, hazard_cur = block_item
    netted = (
        jnp.einsum("tcj,tjp->tcp", fwd_table, spot, precision=HIGHEST_PREC) - dom_table[:, :, None]
    )
    exposure = jnp.maximum(netted, 0.0)
    scale_row = hazard_scale[None, :, None]
    density = jnp.exp(-scale_row * hazard_prev[:, None, :]) - jnp.exp(
        -scale_row * hazard_cur[:, None, :]
    )
    return jnp.sum(exposure * density, axis=2)


def weigh_dates(fwd_table, dom_table, spot, hazard_prev, hazard_cur, hazard_scale):
    date_count, path_count = hazard_cur.shape
    cp_count = dom_table.shape[1]
    ccy_count = spot.shape[1]
    block_dates = math.gcd(date_count, max(1, 32768 // path_count))
    groups = date_count // block_dates
    blocks = (
        fwd_table.reshape(groups, block_dates, cp_count, ccy_count),
        dom_table.reshape(groups, block_dates, cp_count),
        spot.reshape(groups, block_dates, ccy_count, path_count),
        hazard_prev.reshape(groups, block_dates, path_count),
        hazard_cur.reshape(groups, block_dates, path_count),
    )
    weighed = lax.map(lambda block_item: weigh_block(block_item, hazard_scale), blocks)
    return weighed.reshape(date_count, cp_count)


def local_walk(rate_shock, other_shock, fx_vol, fx_corr, date_step, decay_rate, noise_scale):
    date_count = rate_shock.shape[0]
    date_index = jnp.arange(date_count, dtype=jnp.int32)
    date_gap = date_index[:, None] - date_index[None, :]
    is_below = date_gap >= 0
    powers = jnp.where(is_below, decay_rate ** jnp.maximum(date_gap, 0).astype(jnp.float32), 0.0)
    lower_ones = is_below.astype(jnp.float32)
    rate_walk = noise_scale * jnp.dot(powers, rate_shock, precision=HIGHEST_PREC)
    mix_weight = jnp.sqrt(1.0 - fx_corr * fx_corr)
    mixed = fx_corr[:, None, None] * rate_shock[None] + mix_weight[:, None, None] * other_shock
    moves = (fx_vol * math.sqrt(date_step))[:, None, None] * mixed - (
        0.5 * fx_vol * fx_vol * date_step
    )[:, None, None]
    fx_walk = jnp.einsum("ts,jsp->tjp", lower_ones, moves, precision=HIGHEST_PREC)
    carry_gain = decay_rate ** (jnp.arange(date_count, dtype=jnp.float32) + 1.0)
    return (rate_walk, fx_walk, carry_gain, lower_ones)


def path_intensity(rate_walk, carry_gain, rate_in):
    shifted = rate_walk + carry_gain[:, None] * rate_in[None, :] + RATE_SHIFT
    return 0.1 + 0.5 * shifted * shifted


def finish_paths(intensity, lower_ones, fx_walk, hazard_in, log_in, date_step):
    hazard_cur = hazard_in[None, :] + date_step * jnp.dot(
        lower_ones, intensity, precision=HIGHEST_PREC
    )
    hazard_prev = hazard_cur - date_step * intensity
    spot = jnp.exp(fx_walk + log_in[None])
    return (hazard_prev, hazard_cur, spot)


def combine_affine(earlier, later):
    gain_a, end_a, log_a = earlier
    gain_b, end_b, log_b = later
    return (gain_b * gain_a, gain_b * end_a + end_b, log_a + log_b)


def combine_total(earlier, later):
    return earlier + later


def per_device(
    shock_rate,
    shock_fx,
    fx_vol,
    fx_corr,
    hazard_scale,
    counterparty,
    currency,
    maturity,
    notional,
    strike,
):
    local_dates = shock_rate.shape[0]
    total_dates = local_dates * lax.axis_size("tm")
    total_paths = shock_rate.shape[1] * lax.axis_size("path")
    cp_count = hazard_scale.shape[0]
    ccy_count = fx_vol.shape[0]
    date_step = HORIZON / total_dates
    decay_rate = math.exp(-2.0 / total_dates)
    noise_scale = math.sqrt(1.0 - decay_rate * decay_rate)
    first_date = lax.axis_index("tm") * local_dates
    rate_walk, fx_walk, carry_gain, lower_ones = local_walk(
        shock_rate, shock_fx, fx_vol, fx_corr, date_step, decay_rate, noise_scale
    )
    blank = jnp.zeros_like(rate_walk[0])
    span_gain = jnp.full((1,), decay_rate**local_dates, jnp.float32)
    unit_gain = jnp.ones((1,), jnp.float32)
    log_blank = jnp.zeros_like(fx_walk[0])
    carried = carried_in(
        (span_gain, rate_walk[-1], fx_walk[-1]), "tm", combine_affine, (unit_gain, blank, log_blank)
    )
    rate_in, log_in = (carried[1], carried[2])
    intensity = path_intensity(rate_walk, carry_gain, rate_in)
    block_total = date_step * jnp.sum(intensity, axis=0)
    hazard_in = carried_in(block_total, "tm", combine_total, blank)
    hazard_prev, hazard_cur, spot = finish_paths(
        intensity, lower_ones, fx_walk, hazard_in, log_in, date_step
    )
    date_rows = first_date + jnp.arange(local_dates, dtype=jnp.int32)
    fwd_table, dom_table = trade_tables(
        date_rows,
        counterparty,
        currency,
        maturity,
        notional,
        strike,
        cp_count,
        ccy_count,
        date_step,
    )
    local_sum = weigh_dates(fwd_table, dom_table, spot, hazard_prev, hazard_cur, hazard_scale)
    discount = jnp.exp(-RATE_DOM * date_step * (jnp.arange(total_dates, dtype=jnp.float32) + 1.0))
    profile = lax.psum(local_sum, "path") / (total_paths * date_step)
    own_discount = lax.dynamic_slice_in_dim(discount, first_date, local_dates, 0)
    cva = lax.psum(LOSS_SHARE * date_step * jnp.sum(own_discount[:, None] * profile, axis=0), "tm")
    return (profile, cva)


def solution(mesh):
    return jax.shard_map(
        per_device,
        mesh=mesh,
        in_specs=(P("tm", "path"), P(None, "tm", "path"), P(), P(), P(), P(), P(), P(), P(), P()),
        out_specs=(P("tm", None), P()),
        check_vma=False,
    )
```

profile of v0, /device:TPU:0, one launch (start us, length us, event | category | flops | bytes accessed | tf_op | source)
XLA Modules:
  0.0 156.9 jit_solution(9286434855395764987)
XLA Ops:
  7.2 0.0 all-gather.4.cloned.1.call-start
  7.2 0.7 broadcast_multiply_fusion.3
  7.9 5.5 %fusion.8 = f32[16,4,16384]{2,0,1:T(8,128)S(1)} fusion(f32[4,16,16384]{2,1,0:T(8,128)} %param.17, f32[4]{0:T(128)S(1)} %get-tuple-element.248, f32[4]{0:T(128)S(1)} %get-tuple-element.251, f32[16,16384]{1,0:T(8,128)} %param.16, f32[4]{0:T(128)} %param.19, f32[4]{0:T(128)S(1)} %get-tuple-element.247), kind=kOutput, calls=%fused_computation.23 | convolution fusion | flops 206569984 | bytes 9437248 | tf_op jit(solution)/shard_map/ts,jsp->tjp/dot_general | solution.py:92
  13.4 0.0 copy-start
  13.4 1.9 %copy-done = f32[16,4,16384]{2,0,1:T(8,128)} copy-done((f32[16,4,16384]{2,0,1:T(8,128)}, f32[16,4,16384]{2,0,1:T(8,128)S(1)}, u32[]{:S(2)}) %copy-start) | copy-done | bytes 4194328
  15.4 0.0 copy-start.5
  15.4 0.0 copy-start.6
  15.4 0.2 slice.9
  15.6 0.9 copy.15
  16.5 0.0 all-gather.4.cloned.1.call-update
  16.6 0.0 copy-done.1
  16.6 1.0 convolution_multiply_fusion.1
  17.6 0.1 slice_bitcast_fusion
  17.6 10.5 %all-gather.1 = f32[4,1,16384]{2,1,0:T(1,128)S(1)} all-gather(f32[1,1,16384]{2,1,0:T(1,128)S(1)} %slice_bitcast_fusion), channel_id=1, replica_groups=mesh['path'=8,'tm'=4] {'tm'}, dimensions={0}, use_global_device_ids=true | all-gather | bytes 327680 | tf_op jit(solution)/shard_map/all_gather | solution.py:18
  28.1 0.0 copy-done.8
  28.1 0.6 dynamic-slice
  28.7 0.8 dynamic-update-slice
  29.5 8.9 %all-reduce = f32[4]{0:T(128)S(1)} all-reduce(f32[4]{0:T(128)S(1)} %dynamic-update-slice), channel_id=1, replica_groups=mesh['path'=8,'tm'=4] {'tm'}, use_global_device_ids=true, to_apply=%add | all-reduce | flops 4 | bytes 32
  38.4 0.2 copy.24
  38.6 0.0 copy-done.2
  38.6 0.1 dynamic-slice_multiply_fusion
  38.7 0.0 copy-done.5
  38.7 0.0 copy-done.6
  38.8 0.2 fusion.23
  39.0 0.1 fusion.29
  39.1 0.2 fusion.20
  39.3 6.6 %all-gather.4.cloned.1.call-done = f32[4,4,16384]{2,1,0:T(4,128)} async-done(((f32[1,4,16384]{2,1,0:T(4,128)}), f32[4,4,16384]{2,1,0:T(4,128)}) %all-gather.4.cloned.1.call-update) | async-done | bytes 1048592 | tf_op jit(solution)/shard_map/all_gather | solution.py:18
  46.0 2.7 %add_exponential_fusion = f32[16,4,16384]{2,0,1:T(8,128)S(1)} fusion(f32[16,4,16384]{2,0,1:T(8,128)} %copy-done, f32[4,16384]{1,0:T(4,128)S(1)} %get-tuple-element.178), kind=kLoop, calls=%fused_computation.22 | loop fusion | flops 1048576 | bytes 8650752 | tf_op jit(solution)/shard_map/exp | solution.py:107
  48.7 4.6 %copy.18 = f32[16,4,16384]{2,1,0:T(4,128)} copy(f32[16,4,16384]{2,0,1:T(8,128)S(1)} %add_exponential_fusion) | data formatting | bytes 8388608 | tf_op jit(solution)/shard_map/while | solution.py:75
  53.4 0.4 fusion.66
  53.8 15.0 %all-gather = f32[65536]{0:T(1024)S(1)} all-gather(f32[16384]{0:T(1024)S(1)} %broadcast_multiply_fusion), channel_id=2, replica_groups=mesh['path'=8,'tm'=4] {'tm'}, dimensions={0}, use_global_device_ids=true | all-gather | bytes 327680 | tf_op jit(solution)/shard_map/all_gather | solution.py:18
  68.8 0.1 reshape.72
  68.9 0.2 while.37
  69.1 2.1 %multiply_subtract_fusion = (f32[16,16384]{1,0:T(8,128)}, f32[16,16384]{1,0:T(8,128)S(1)}) fusion(f32[16,16384]{1,0:T(8,128)S(1)} %convolution_multiply_fusion.1, f32[16384]{0:T(1024)S(1)} %get-tuple-element.179, f32[16]{0:T(128)S(1)} %add_power_fusion, f32[16384]{0:T(1024)S(1)} %get-tuple-element.180), kind=kOutput, calls=%fused_computation.36 | convolution fusion | flops 54526464 | bytes 3276864 | tf_op jit(solution)/shard_map/dot_general | solution.py:103
  71.2 1.8 %reshape.69 = f32[8,2,16384]{2,1,0:T(2,128)S(1)} reshape(f32[16,16384]{1,0:T(8,128)} %get-tuple-element.249) | data formatting | bytes 2097152 | tf_op jit(solution)/shard_map/reshape | solution.py:72
  73.1 0.6 reshape.70
  73.7 51.0 %while.38 = (s32[]{:T(128)}, f32[8,2,32]{2,1,0:T(2,128)S(1)}, f32[8,2,32,4]{2,1,0,3:T(2,128)S(1)}, f32[8,2,4,16384]{3,2,1,0:T(4,128)}, f32[8,2,32]{2,1,0:T(2,128...) while((s32[]{:T(128)}, f32[8,2,32]{2,1,0:T(2,128)S(1)}, ...), condition=%wide.region_7.8_spmd, body=%wide.region_5.7_spmd.sunk | while | flops 57671616 | bytes 1317113 | solution.py:75
  73.8 6.3 %fusion.73 = f32[2,32]{1,0:T(2,128)S(1)} fusion(f32[2,16384]{1,0:T(2,128)S(1)} %get-tuple-element.373, f32[2,16384]{1,0:T(2,128)S(1)} %get-tuple-element.374, f32[32]{0:T(128)S(1)} %bitcast.77, f32[2,32]{1,0:T(2,128)S(1)} %fusion.72, f32[8,2,4,16384]{3,2,1,0:T(4,128)} %get-tuple-element.447, s32[]{:T(128)S(6)} %copy.46, ...), kind=kOutput, calls=%fused_computation.8.clone.1 | convolution fusion | flops 57671616 | bytes 788100 | tf_op jit(solution)/shard_map/while/body/eval_jaxpr/tcj,tjp->tcp/dot_general | solution.py:52
  80.1 6.3 %fusion.73 = f32[2,32]{1,0:T(2,128)S(1)} fusion(f32[2,16384]{1,0:T(2,128)S(1)} %get-tuple-element.373, f32[2,16384]{1,0:T(2,128)S(1)} %get-tuple-element.374, f32[32]{0:T(128)S(1)} %bitcast.77, f32[2,32]{1,0:T(2,128)S(1)} %fusion.72, f32[8,2,4,16384]{3,2,1,0:T(4,128)} %get-tuple-element.447, s32[]{:T(128)S(6)} %copy.46, ...), kind=kOutput, calls=%fused_computation.8.clone.1 | convolution fusion | flops 57671616 | bytes 788100 | tf_op jit(solution)/shard_map/while/body/eval_jaxpr/tcj,tjp->tcp/dot_general | solution.py:52
  86.5 6.3 %fusion.73 = f32[2,32]{1,0:T(2,128)S(1)} fusion(f32[2,16384]{1,0:T(2,128)S(1)} %get-tuple-element.373, f32[2,16384]{1,0:T(2,128)S(1)} %get-tuple-element.374, f32[32]{0:T(128)S(1)} %bitcast.77, f32[2,32]{1,0:T(2,128)S(1)} %fusion.72, f32[8,2,4,16384]{3,2,1,0:T(4,128)} %get-tuple-element.447, s32[]{:T(128)S(6)} %copy.46, ...), kind=kOutput, calls=%fused_computation.8.clone.1 | convolution fusion | flops 57671616 | bytes 788100 | tf_op jit(solution)/shard_map/while/body/eval_jaxpr/tcj,tjp->tcp/dot_general | solution.py:52
  92.9 6.3 %fusion.73 = f32[2,32]{1,0:T(2,128)S(1)} fusion(f32[2,16384]{1,0:T(2,128)S(1)} %get-tuple-element.373, f32[2,16384]{1,0:T(2,128)S(1)} %get-tuple-element.374, f32[32]{0:T(128)S(1)} %bitcast.77, f32[2,32]{1,0:T(2,128)S(1)} %fusion.72, f32[8,2,4,16384]{3,2,1,0:T(4,128)} %get-tuple-element.447, s32[]{:T(128)S(6)} %copy.46, ...), kind=kOutput, calls=%fused_computation.8.clone.1 | convolution fusion | flops 57671616 | bytes 788100 | tf_op jit(solution)/shard_map/while/body/eval_jaxpr/tcj,tjp->tcp/dot_general | solution.py:52
  99.2 6.3 %fusion.73 = f32[2,32]{1,0:T(2,128)S(1)} fusion(f32[2,16384]{1,0:T(2,128)S(1)} %get-tuple-element.373, f32[2,16384]{1,0:T(2,128)S(1)} %get-tuple-element.374, f32[32]{0:T(128)S(1)} %bitcast.77, f32[2,32]{1,0:T(2,128)S(1)} %fusion.72, f32[8,2,4,16384]{3,2,1,0:T(4,128)} %get-tuple-element.447, s32[]{:T(128)S(6)} %copy.46, ...), kind=kOutput, calls=%fused_computation.8.clone.1 | convolution fusion | flops 57671616 | bytes 788100 | tf_op jit(solution)/shard_map/while/body/eval_jaxpr/tcj,tjp->tcp/dot_general | solution.py:52
  105.6 6.3 %fusion.73 = f32[2,32]{1,0:T(2,128)S(1)} fusion(f32[2,16384]{1,0:T(2,128)S(1)} %get-tuple-element.373, f32[2,16384]{1,0:T(2,128)S(1)} %get-tuple-element.374, f32[32]{0:T(128)S(1)} %bitcast.77, f32[2,32]{1,0:T(2,128)S(1)} %fusion.72, f32[8,2,4,16384]{3,2,1,0:T(4,128)} %get-tuple-element.447, s32[]{:T(128)S(6)} %copy.46, ...), kind=kOutput, calls=%fused_computation.8.clone.1 | convolution fusion | flops 57671616 | bytes 788100 | tf_op jit(solution)/shard_map/while/body/eval_jaxpr/tcj,tjp->tcp/dot_general | solution.py:52
  112.0 6.3 %fusion.73 = f32[2,32]{1,0:T(2,128)S(1)} fusion(f32[2,16384]{1,0:T(2,128)S(1)} %get-tuple-element.373, f32[2,16384]{1,0:T(2,128)S(1)} %get-tuple-element.374, f32[32]{0:T(128)S(1)} %bitcast.77, f32[2,32]{1,0:T(2,128)S(1)} %fusion.72, f32[8,2,4,16384]{3,2,1,0:T(4,128)} %get-tuple-element.447, s32[]{:T(128)S(6)} %copy.46, ...), kind=kOutput, calls=%fused_computation.8.clone.1 | convolution fusion | flops 57671616 | bytes 788100 | tf_op jit(solution)/shard_map/while/body/eval_jaxpr/tcj,tjp->tcp/dot_general | solution.py:52
  118.3 6.3 %fusion.73 = f32[2,32]{1,0:T(2,128)S(1)} fusion(f32[2,16384]{1,0:T(2,128)S(1)} %get-tuple-element.373, f32[2,16384]{1,0:T(2,128)S(1)} %get-tuple-element.374, f32[32]{0:T(128)S(1)} %bitcast.77, f32[2,32]{1,0:T(2,128)S(1)} %fusion.72, f32[8,2,4,16384]{3,2,1,0:T(4,128)} %get-tuple-element.447, s32[]{:T(128)S(6)} %copy.46, ...), kind=kOutput, calls=%fused_computation.8.clone.1 | convolution fusion | flops 57671616 | bytes 788100 | tf_op jit(solution)/shard_map/while/body/eval_jaxpr/tcj,tjp->tcp/dot_general | solution.py:52
  124.7 15.0 %psum.14 = f32[16,32]{1,0:T(8,128)S(1)} all-reduce(f32[16,32]{1,0:T(8,128)S(1)} %bitcast.74), channel_id=1, replica_groups=mesh['path'=8,'tm'=4] {'path'}, use_global_device_ids=true, to_apply=%region_8.9 | all-reduce | flops 512 | bytes 4096 | tf_op jit(solution)/shard_map/psum | solution.py:173
  139.7 0.6 multiply_reduce_fusion
  140.3 9.7 %psum.15 = f32[32]{0:T(128)} all-reduce(f32[32]{0:T(128)S(1)} %broadcast_multiply_fusion.2), channel_id=1, replica_groups=mesh['path'=8,'tm'=4] {'tm'}, use_global_device_ids=true, to_apply=%region_10.11 | all-reduce | flops 32 | bytes 256 | tf_op jit(solution)/shard_map/psum | solution.py:175
  (55 shorter events, 0.5 us)
Async XLA Ops:
  7.2 38.8 %all-gather.4.cloned.1.call-start = ((), (), s32[]{:S(2)}) async-start(), calls=%async_computation | async-start | bytes 1310720 | tf_op jit(solution)/shard_map/all_gather | solution.py:18
  7.9 8.7 %copy-start.1 = (f32[16,16384]{1,0:T(8,128)S(1)}, f32[16,16384]{1,0:T(8,128)}, u32[]{:S(2)}) copy-start(f32[16,16384]{1,0:T(8,128)} %param.16) | copy-start | bytes 3145732
  7.9 20.2 %copy-start.8 = (u32[32]{0:T(128)S(1)}, u32[32]{0:T(128)}, u32[]{:S(2)}) copy-start(u32[32]{0:T(128)} %constant.112) | copy-start | bytes 388
  13.4 1.9 %copy-start = (f32[16,4,16384]{2,0,1:T(8,128)}, f32[16,4,16384]{2,0,1:T(8,128)S(1)}, u32[]{:S(2)}) copy-start(f32[16,4,16384]{2,0,1:T(8,128)S(1)} %fusion.8) | copy-start | bytes 12582916
  15.4 23.2 %copy-start.2 = (f32[512]{0:T(512)S(1)}, f32[512]{0:T(512)}, u32[]{:S(2)}) copy-start(f32[512]{0:T(512)} %param.24) | copy-start | bytes 6148
  15.4 23.2 %copy-start.3 = (f32[512]{0:T(512)S(1)}, f32[512]{0:T(512)}, u32[]{:S(2)}) copy-start(f32[512]{0:T(512)} %param.25) | copy-start | bytes 6148
  15.4 23.4 %copy-start.7 = (f32[32]{0:T(128)S(1)}, f32[32]{0:T(128)}, u32[]{:S(2)}) copy-start(f32[32]{0:T(128)} %param.20) | copy-start | bytes 388
  15.4 23.4 %copy-start.4 = (s32[512]{0:T(512)S(1)}, s32[512]{0:T(512)}, u32[]{:S(2)}) copy-start(s32[512]{0:T(512)} %param.22) | copy-start | bytes 6148
  15.4 23.4 %copy-start.5 = (s32[512]{0:T(512)S(1)}, s32[512]{0:T(512)}, u32[]{:S(2)}) copy-start(s32[512]{0:T(512)} %param.23) | copy-start | bytes 6148
  15.4 23.4 %copy-start.6 = (s32[512]{0:T(512)S(1)}, s32[512]{0:T(512)}, u32[]{:S(2)}) copy-start(s32[512]{0:T(512)} %param.21) | copy-start | bytes 6148
Sparse Core Ops, SparseCore 0:
  16.7 29.2 all-gather.3
where the time goes:
time: 157 us
  matrix products  59.4 us (38%)
  blocking collectives  59.1 us (38%)
  between operations  14.3 us (9%)
  local copies, waits for them, and re-layouts  12.3 us (8%)
  waiting for transfers between devices  6.65 us (4%)
  other arithmetic  4.69 us (3%)
    dot_general x8, matrix products, weigh_block(): jnp.einsum('tcj,tjp->tcp', fwd_table, spot, precision=HIGHEST_PREC)  50.4 us
    all_gather x2, blocking collectives, carried_in(): gathered = jax.tree.map(lambda a: lax.all_gather(a, axis), part)  25.5 us
    psum x1, blocking collectives, per_device(): profile = lax.psum(local_sum, 'path') / (total_paths * date_step)  15 us
    psum x1, blocking collectives, per_device(): lax.psum(LOSS_SHARE * date_step * jnp.sum(own_discount[:, None] * profile...  9.71 us
    unnamed x1, blocking collectives  8.93 us
    all_gather x1, waiting for transfers between devices, carried_in(): gathered = jax.tree.map(lambda a: lax.all_gather(a, axis), part)  6.64 us
    dot_general x1, matrix products, local_walk(): jnp.einsum('ts,jsp->tjp', lower_ones, moves, precision=HIGHEST_PREC)  5.52 us
    while x1, local copies, waits for them, and re-layouts, weigh_dates(): lax.map(lambda block_item: weigh_block(block_item, hazard_scale), blocks)  4.63 us
  transfers between devices with their start and end apart: 1, of which 1 were waited for; matrix products, arithmetic and copies ran while one was open for 2% of the time, Pallas kernels for 0%

commit v1 on v0

v1 whole, which is shorter than its diff:
```python
import functools
import math

import jax
import jax.numpy as jnp
from jax import lax
from jax.experimental import pallas as pl
from jax.experimental.pallas import tpu as pltpu
from jax.sharding import PartitionSpec as P

HORIZON = 5.0
RATE_DOM = 0.03
RATE_FOR = 0.01
LOSS_SHARE = 0.6
RATE_SHIFT = 1.5
BASE_INTENSITY = 0.1
LOG2E = math.log2(math.e)
HIGHEST = lax.Precision.HIGHEST
MESH = pl.DeviceIdType.MESH
F32 = jnp.float32
BF16 = jnp.bfloat16

CHUNKS = 8
WALK_BLOCK = 512
MAIN_BLOCK = 256


def iota(shape, dim):
    return lax.broadcasted_iota(jnp.int32, shape, dim)


def halves(x):
    top = x.astype(BF16)
    return top, (x - top.astype(F32)).astype(BF16)


def pick(index, values):
    out = jnp.zeros(index.shape, F32)
    for place, value in values:
        out = jnp.where(index == place, value, out)
    return out


def kernel(
    sizes,
    vol_ref,
    corr_ref,
    scale_ref,
    party_ref,
    ccy_ref,
    mat_ref,
    notional_ref,
    strike_ref,
    rate_hbm,
    fx_hbm,
    profile_ref,
    cva_ref,
    rate_in,
    fx_in,
    walk,
    coef,
    table,
    pay,
    recv,
    state,
    inten,
    acc,
    scale_col,
    bias_col,
    row_out,
    row_recv,
    cva_out,
    cva_recv,
    in_sem,
    send_sem,
    recv_sem,
    row_send_sem,
    row_recv_sem,
    cva_send_sem,
    cva_recv_sem,
):
    dates, paths, nccy, ncp, n_tm, n_path, total_dates, total_paths = sizes
    rounds = n_tm.bit_length() - 1
    chunk = paths // CHUNKS
    dt = HORIZON / total_dates
    lam = 2.0 / total_dates
    decay = math.exp(-lam)
    noise = math.sqrt(1.0 - decay * decay)
    gains = [decay ** (dates << k) for k in range(rounds)]
    quads = [
        0.5 * dt * sum(decay ** (2 * (t + 1)) for t in range(dates << k)) for k in range(rounds)
    ]
    shift = dates.bit_length() - 1
    walk_rows = (nccy + 1) * dates
    fx_rows = nccy * dates

    tm = lax.axis_index("tm")
    me = lax.axis_index("path")
    first_date = tm * dates

    def fetch(c):
        cols = pl.ds(pl.multiple_of(c * chunk, chunk), chunk)
        return (
            pltpu.make_async_copy(rate_hbm.at[:, cols], rate_in.at[:, cols], in_sem.at[0, c]),
            pltpu.make_async_copy(fx_hbm.at[:, :, cols], fx_in.at[:, :, cols], in_sem.at[1, c]),
        )

    for c in range(CHUNKS):
        for copy in fetch(c):
            copy.start()

    barrier = pltpu.get_barrier_semaphore()
    for step in range(1, n_tm):
        other = lax.rem(tm + step, n_tm)
        pl.semaphore_signal(barrier, inc=1, device_id=(me, other), device_id_type=MESH)
    for step in range(1, n_path):
        other = lax.rem(me + step, n_path)
        pl.semaphore_signal(barrier, inc=1, device_id=(other, tm), device_id_type=MESH)

    width = 3 * walk_rows
    shape = (walk_rows + 16, width)
    row = iota(shape, 0)
    col = iota(shape, 1)
    is_walk = row < walk_rows
    blk = jnp.where(is_walk, row >> shift, row - walk_rows)
    day = jnp.where(is_walk, row & (dates - 1), dates - 1)
    base = jnp.where(
        col >= 2 * walk_rows,
        col - 2 * walk_rows,
        jnp.where(col >= walk_rows, col - walk_rows, col),
    )
    src = base >> shift
    src_day = base & (dates - 1)
    vol = pick(blk, [(j + 1, vol_ref[j]) for j in range(nccy)]) * (math.sqrt(dt) * LOG2E)
    corr = pick(blk, [(j + 1, corr_ref[j]) for j in range(nccy)])
    below = src_day <= day
    gap = jnp.maximum(day - src_day, 0).astype(F32)
    back = src_day.astype(F32)
    value = jnp.where(
        src == 0,
        jnp.where(blk == 0, noise * jnp.exp(-lam * gap), vol * corr),
        jnp.where(src == blk, vol * jnp.sqrt(1.0 - corr * corr), 0.0),
    )
    value = jnp.where(below, value, 0.0)
    slope = (dt / noise) * (jnp.exp(-lam * (back + 1.0)) - jnp.exp(-lam * (2 * dates + 1 - back)))
    value = jnp.where(blk == nccy + 1, jnp.where(src == 0, slope, 0.0), value)
    value = jnp.where(blk > nccy + 1, 0.0, value)
    top, low = halves(value)
    coef[...] = jnp.where(col < 2 * walk_rows, top.astype(F32), low.astype(F32)).astype(BF16)

    prow = iota((8, 128), 0)
    slope_row, quad_row = nccy + 1, nccy + 2
    slope_const = RATE_SHIFT * dt * sum(decay ** (t + 1) for t in range(dates))
    const_rows = pick(prow, [(slope_row, slope_const), (quad_row, BASE_INTENSITY * dt * dates)])

    def wide(rows, count):
        return jnp.concatenate([rows] * (count // 128), axis=1) if count > 128 else rows

    def send(k, c):
        partner = tm ^ (1 << k)
        return pltpu.make_async_remote_copy(
            src_ref=pay.at[k, c],
            dst_ref=recv.at[k, c],
            send_sem=send_sem.at[k, c],
            recv_sem=recv_sem.at[k, c],
            device_id=(me, partner),
            device_id_type=MESH,
        )

    def bit(k):
        return (tm >> k) & 1

    last = rounds - 1

    def start_round(k, c):
        if k < last:
            send(k, c).start()
        else:

            @pl.when(bit(k) == 0)
            def _():
                send(k, c).start()

    def wait_round(k, c):
        if k < last:
            send(k, c).wait_recv()
        else:

            @pl.when(bit(k) == 1)
            def _():
                send(k, c).wait_recv()

    def walk_part(c, first):
        at = c * chunk + first
        cols = pl.ds(pl.multiple_of(at, WALK_BLOCK), WALK_BLOCK)
        x = jnp.concatenate(
            [rate_in[:, cols]] + [fx_in[j, :, cols] for j in range(nccy)], axis=0
        )
        top, low = halves(x)
        out = jnp.dot(
            coef[...], jnp.concatenate([top, low, top], axis=0), preferred_element_type=F32
        )
        walk[:, cols] = out[:walk_rows]
        shifted = out[:dates] + RATE_SHIFT
        square = jnp.sum(shifted * shifted, axis=0, keepdims=True) * (0.5 * dt)
        is_quad = wide(prow, WALK_BLOCK) == quad_row
        ends = out[walk_rows : walk_rows + 8] + wide(const_rows, WALK_BLOCK)
        ends = ends + jnp.where(is_quad, square, 0.0)
        pay[0, c, :, pl.ds(pl.multiple_of(first, WALK_BLOCK), WALK_BLOCK)] = ends

    def walk_chunk(c, carry):
        for copy in fetch(c):
            copy.wait()

        def one(b, carry):
            walk_part(c, b * WALK_BLOCK)
            return carry

        lax.fori_loop(0, chunk // WALK_BLOCK, one, 0)

        if rounds:
            start_round(0, c)
        return carry

    if rounds:

        @pl.when(bit(last) == 0)
        def _():
            recv[last] = jnp.zeros(recv.shape[1:], F32)

    pl.semaphore_wait(barrier, n_tm - 1 + n_path - 1)
    lax.fori_loop(0, CHUNKS, walk_chunk, 0)

    party = party_ref[...]
    expiry = mat_ref[...]
    ntrade = party.shape[1]
    member = jnp.where(iota((ncp, ntrade), 0) == party, 1.0, 0.0).astype(F32)
    date = first_date + iota((dates, ntrade), 0)
    alive = date < expiry
    left = (expiry - date).astype(F32) * dt
    w_for = jnp.where(alive, notional_ref[...] * jnp.exp(-RATE_FOR * left), 0.0)
    w_dom = jnp.where(
        alive, -(notional_ref[...] * strike_ref[...]) * jnp.exp(-RATE_DOM * left), 0.0
    )
    by_ccy = [jnp.where(ccy_ref[...] == j, w_for, 0.0) for j in range(nccy)]
    sums = lax.dot_general(
        member,
        jnp.concatenate(by_ccy * 3 + [w_dom] * 3, axis=0),
        (((1,), (1,)), ((), ())),
        precision=HIGHEST,
        preferred_element_type=F32,
    )
    tcol = iota(sums.shape, 1)
    top = sums.astype(BF16).astype(F32)
    low = (sums - top).astype(BF16).astype(F32)
    rest = sums - top - low
    use_low = ((tcol >= 2 * fx_rows) & (tcol < 3 * fx_rows)) | (
        (tcol >= 3 * fx_rows + dates) & (tcol < 3 * fx_rows + 2 * dates)
    )
    use_rest = tcol >= 3 * fx_rows + 2 * dates
    parts = jnp.where(use_rest, rest, jnp.where(use_low, low, top))
    for t in range(dates):
        table[t * ncp : (t + 1) * ncp, :] = jnp.where(
            (tcol & (dates - 1)) == t, parts, 0.0
        ).astype(BF16)

    crow = iota((ncp, 128), 0)
    scale_col[...] = pick(crow, [(c, scale_ref[c]) for c in range(ncp)]) * (-LOG2E)
    brow = iota((fx_rows, 128), 0)
    bvol = pick(brow >> shift, [(j, vol_ref[j]) for j in range(nccy)])
    bday = (first_date + (brow & (dates - 1)) + 1).astype(F32)
    bias_col[...] = (-0.5 * dt * LOG2E) * bvol * bvol * bday
    acc[...] = jnp.zeros_like(acc)

    def join(k, c):
        mine, theirs = pay[k - 1, c], recv[k - 1, c]
        upper_is_mine = bit(k - 1) == 1
        lower = jnp.where(upper_is_mine, theirs, mine)
        upper = jnp.where(upper_is_mine, mine, theirs)
        gain, quad = gains[k - 1], quads[k - 1]
        rows = wide(prow, chunk)
        end = lower[0:1]
        total = lower * jnp.where(rows == 0, gain, 1.0) + upper * jnp.where(
            rows == slope_row, gain, 1.0
        )
        extra = upper[slope_row : slope_row + 1] * end + quad * end * end
        total = total + jnp.where(rows == slope_row, (2.0 * quad * gain) * end, 0.0)
        total = total + jnp.where(rows == quad_row, extra, 0.0)
        pay[k, c] = total

    def absorb(c):
        now = jnp.zeros((8, chunk), F32)
        rows = wide(prow, chunk)
        for k in reversed(range(rounds)):
            other = recv[k, c]
            end = now[0:1]
            extra = other[slope_row : slope_row + 1] * end + quads[k] * end * end
            then = now * jnp.where(rows == 0, gains[k], 1.0) + other
            then = then + jnp.where(rows == quad_row, extra, 0.0)
            now = then if k == last else jnp.where(bit(k) == 1, then, now)
        state[...] = now

    carry_gain = jnp.exp(-lam * (iota((dates, 128), 0).astype(F32) + 1.0))
    ones = jnp.ones((3 * dates, MAIN_BLOCK), BF16)

    def main_part(c, first):
        at = c * chunk + first
        cols = pl.ds(pl.multiple_of(at, MAIN_BLOCK), MAIN_BLOCK)
        own = pl.ds(pl.multiple_of(first, MAIN_BLOCK), MAIN_BLOCK)
        start = state[:, own]
        shifted = walk[:dates, cols] + wide(carry_gain, MAIN_BLOCK) * start[0:1] + RATE_SHIFT
        inten[...] = (BASE_INTENSITY * dt) + (0.5 * dt) * (shifted * shifted)
        spots = []
        for j in range(nccy):
            log = walk[(j + 1) * dates : (j + 2) * dates, cols] + start[j + 1 : j + 2]
            log = log + wide(bias_col[j * dates : (j + 1) * dates], MAIN_BLOCK)
            spots.append(jnp.exp2(log))
        top, low = halves(jnp.concatenate(spots, axis=0))
        netted = jnp.dot(
            table[...],
            jnp.concatenate([top, low, top, ones], axis=0),
            preferred_element_type=F32,
        )
        scales = wide(scale_col[...], MAIN_BLOCK)
        hazard = start[quad_row : quad_row + 1]
        before = jnp.exp2(scales * hazard)
        for t in range(dates):
            hazard = hazard + inten[t : t + 1, :]
            after = jnp.exp2(scales * hazard)
            part = slice(t * ncp, (t + 1) * ncp)
            term = jnp.maximum(netted[part], 0.0) * (before - after)
            total = acc[part]
            for i in range(MAIN_BLOCK // 128):
                total = total + term[:, i * 128 : (i + 1) * 128]
            acc[part] = total
            before = after

    def main_chunk(c, carry):
        for k in range(1, rounds):
            wait_round(k - 1, c)
            if k < last:
                join(k, c)
                start_round(k, c)
            else:

                @pl.when(bit(k) == 0)
                def _():
                    join(k, c)
                    send(k, c).start()

        if rounds:
            wait_round(last, c)
        absorb(c)

        def one(b, carry):
            main_part(c, b * MAIN_BLOCK)
            return carry

        lax.fori_loop(0, chunk // MAIN_BLOCK, one, 0)
        return carry

    lax.fori_loop(0, CHUNKS, main_chunk, 0)

    local = lax.dot_general(
        jnp.ones((8, 128), F32),
        acc[...],
        (((1,), (1,)), ((), ())),
        precision=HIGHEST,
        preferred_element_type=F32,
    )
    row_out[...] = local[0:1]
    row_recv[me] = local[0:1]

    def row_send(step):
        other = lax.rem(me + step, n_path)
        return pltpu.make_async_remote_copy(
            src_ref=row_out,
            dst_ref=row_recv.at[me],
            send_sem=row_send_sem.at[step],
            recv_sem=row_recv_sem.at[step],
            device_id=(other, tm),
            device_id_type=MESH,
        )

    for step in range(1, n_path):
        row_send(step).start()
    for step in range(1, n_path):
        row_send(step).wait_recv()
    total = row_recv[0]
    for i in range(1, n_path):
        total = total + row_recv[i]
    profile = total * (1.0 / (total_paths * dt))
    profile_ref[...] = profile

    lane = iota((1, dates * ncp), 1)
    day = (first_date + lax.div(lane, ncp) + 1).astype(F32)
    weighed = (LOSS_SHARE * dt) * jnp.exp(-RATE_DOM * dt * day) * profile
    folded = weighed[:, :128]
    for i in range(1, dates * ncp // 128):
        folded = folded + weighed[:, i * 128 : (i + 1) * 128]
    cva_out[...] = folded
    cva_recv[tm] = folded

    def cva_send(step):
        other = lax.rem(tm + step, n_tm)
        return pltpu.make_async_remote_copy(
            src_ref=cva_out,
            dst_ref=cva_recv.at[tm],
            send_sem=cva_send_sem.at[step],
            recv_sem=cva_recv_sem.at[step],
            device_id=(me, other),
            device_id_type=MESH,
        )

    for step in range(1, n_tm):
        cva_send(step).start()
    for step in range(1, n_tm):
        cva_send(step).wait_recv()
    total = cva_recv[0]
    for i in range(1, n_tm):
        total = total + cva_recv[i]
    cva = total
    for i in range(1, 128 // ncp):
        cva = cva + pltpu.roll(total, i * ncp, 1)
    cva_ref[...] = cva

    def drain(c, carry):
        for k in range(rounds):
            if k < last:
                send(k, c).wait_send()
            else:

                @pl.when(bit(k) == 0)
                def _():
                    send(k, c).wait_send()

        return carry

    lax.fori_loop(0, CHUNKS, drain, 0)
    for step in range(1, n_path):
        row_send(step).wait_send()
    for step in range(1, n_tm):
        cva_send(step).wait_send()


def per_device(
    shock_rate,
    shock_fx,
    fx_vol,
    fx_corr,
    hazard_scale,
    counterparty,
    currency,
    maturity,
    notional,
    strike,
):
    dates, paths = shock_rate.shape
    nccy = shock_fx.shape[0]
    ncp = hazard_scale.shape[0]
    n_tm = lax.axis_size("tm")
    n_path = lax.axis_size("path")
    rounds = n_tm.bit_length() - 1
    chunk = paths // CHUNKS
    walk_rows = (nccy + 1) * dates
    smem = pl.BlockSpec(memory_space=pltpu.SMEM)
    vmem = pl.BlockSpec(memory_space=pltpu.VMEM)
    hbm = pl.BlockSpec(memory_space=pl.ANY)
    sizes = (dates, paths, nccy, ncp, n_tm, n_path, dates * n_tm, paths * n_path)
    dma = pltpu.SemaphoreType.DMA
    profile, cva = pl.pallas_call(
        functools.partial(kernel, sizes),
        out_shape=(
            jax.ShapeDtypeStruct((1, dates * ncp), F32),
            jax.ShapeDtypeStruct((1, 128), F32),
        ),
        in_specs=[smem] * 3 + [vmem] * 5 + [hbm] * 2,
        out_specs=(vmem, vmem),
        scratch_shapes=[
            pltpu.VMEM((dates, paths), F32),
            pltpu.VMEM((nccy, dates, paths), F32),
            pltpu.VMEM((walk_rows, paths), F32),
            pltpu.VMEM((walk_rows + 16, 3 * walk_rows), BF16),
            pltpu.VMEM((dates * ncp, 3 * walk_rows), BF16),
            pltpu.VMEM((max(rounds, 1), CHUNKS, 8, chunk), F32),
            pltpu.VMEM((max(rounds, 1), CHUNKS, 8, chunk), F32),
            pltpu.VMEM((8, chunk), F32),
            pltpu.VMEM((dates, MAIN_BLOCK), F32),
            pltpu.VMEM((dates * ncp, 128), F32),
            pltpu.VMEM((ncp, 128), F32),
            pltpu.VMEM((nccy * dates, 128), F32),
            pltpu.VMEM((1, dates * ncp), F32),
            pltpu.VMEM((n_path, 1, dates * ncp), F32),
            pltpu.VMEM((1, 128), F32),
            pltpu.VMEM((n_tm, 1, 128), F32),
            dma((2, CHUNKS)),
            dma((max(rounds, 1), CHUNKS)),
            dma((max(rounds, 1), CHUNKS)),
            dma((n_path,)),
            dma((n_path,)),
            dma((n_tm,)),
            dma((n_tm,)),
        ],
        compiler_params=pltpu.CompilerParams(collective_id=0, has_side_effects=True),
    )(
        fx_vol,
        fx_corr,
        hazard_scale,
        counterparty[None],
        currency[None],
        maturity[None],
        notional[None],
        strike[None],
        shock_rate,
        shock_fx,
    )
    return (profile.reshape(dates, ncp), cva[0, :ncp])


def solution(mesh):
    return jax.shard_map(
        per_device,
        mesh=mesh,
        in_specs=(P("tm", "path"), P(None, "tm", "path"), P(), P(), P(), P(), P(), P(), P(), P()),
        out_specs=(P("tm", None), P()),
        check_vma=False,
    )
```

time: 157 us -> 45.7 us (0.29)
  matrix products: 59.4 us -> 0 us
  blocking collectives: 59.1 us -> 0 us
  Pallas kernels: 0 us -> 41.3 us
  between operations: 14.3 us -> 0.64 us
  local copies, waits for them, and re-layouts: 12.3 us -> 2.29 us
  waiting for transfers between devices: 6.65 us -> 0 us
  other arithmetic: 4.69 us -> 1.34 us
    dot_general x13 -> x0, matrix products: 59.4 us -> none  [the longest x8 50.4 us: weigh_block(): jnp.einsum('tcj,tjp->tcp', fwd_table, spot, precision=HIGHEST_PREC)]
    pallas_call x0 -> x1, Pallas kernels: none -> 41.3 us  [per_device(): pl.pallas_call(functools.partial(kernel, sizes), out_shape=(jax.ShapeDtyp...]
    all_gather x2 -> x0, blocking collectives: 25.5 us -> none  [carried_in(): gathered = jax.tree.map(lambda a: lax.all_gather(a, axis), part)]
    psum x2 -> x0, blocking collectives: 24.8 us -> none  [the longest x1 15 us: per_device(): profile = lax.psum(local_sum, 'path') / (total_paths * date_step)]
    unnamed x1 -> x0, blocking collectives: 8.93 us -> none
    all_gather x1 -> x0, waiting for transfers between devices: 6.64 us -> none  [carried_in(): gathered = jax.tree.map(lambda a: lax.all_gather(a, axis), part)]
    while x1 -> x0, local copies, waits for them, and re-layouts: 4.63 us -> none  [weigh_dates(): lax.map(lambda block_item: weigh_block(block_item, hazard_scale), blocks)]
    unnamed x23 -> x0, local copies, waits for them, and re-layouts: 3.53 us -> none
  transfers between devices with their start and end apart: 1 -> 0, of which waited for: 1 -> 0; matrix products, arithmetic and copies ran while one was open for 2% -> 0% of each run, Pallas kernels for 0% -> 0%
where the time goes in v1:
time: 45.7 us; the launch traced here: 45.6 us
  Pallas kernels  41.3 us (90%)
  local copies, waits for them, and re-layouts  2.29 us (5%)
  other arithmetic  1.34 us (3%)
  between operations  0.64 us (1%)
    pallas_call x1, Pallas kernels, per_device(): pl.pallas_call(functools.partial(kernel, sizes), out_shape=(jax.ShapeDtyp...  41.3 us
    pallas_call x1, other arithmetic, per_device(): pl.pallas_call(functools.partial(kernel, sizes), out_shape=(jax.ShapeDtyp...  1.34 us
    squeeze x1, local copies, waits for them, and re-layouts, per_device(): return (profile.reshape(dates, ncp), cva[0, :ncp])  1.11 us

profile of v1, /device:TPU:0, one launch (start us, length us, event | category | flops | bytes accessed | tf_op | source)
XLA Modules:
  0.0 45.6 jit_solution(3988388849124391489)
XLA Ops:
  0.6 41.3 %shard_map.113 = (f32[1,512]{1,0:T(1,128)}, f32[1,128]{1,0:T(1,128)}) custom-call(f32[4]{0:T(128)} %vol_ref.1, f32[4]{0:T(128)} %corr_ref.1, f32[32]{0:T(128)} %scale_ref.1, s32[1,512]{1,0:T(1,128)} %bitcast.7, s32[1,512]{1,0:T(1,128)} %bitcast.8, s32[1,512]{1,0:T(1,128)} %bitcast.9, f32[1,512]{1,0:T(1,128)} %bitcast.10, f32[1,512]{1,0:T(1,128)} %bitcast.11, ...), custom_call_target="tpu_custom_call" | custom-call | tf_op jit(solution)/shard_map/pallas_call | solution.py:471
  41.9 0.5 %broadcast.3 = f32[]{:T(128)} broadcast(f32[]{:T(128)} %constant.3), dimensions={} | broadcast | bytes 8 | tf_op jit(solution)/shard_map/pallas_call | solution.py:471
  42.4 1.3 %reduce.3 = f32[512]{0:T(512)S(1)} reduce(f32[1,512]{1,0:T(1,128)} %get-tuple-element.4, f32[]{:T(128)} %broadcast.3), dimensions={0}, to_apply=%get-tuple-element.4.reduce_sub_computation.3 | reduce | bytes 4100 | tf_op jit(solution)/shard_map/pallas_call | solution.py:471
  43.8 1.1 %slice_bitcast_fusion = f32[32]{0:T(128)} fusion(f32[1,128]{1,0:T(1,128)} %get-tuple-element.5), kind=kLoop, calls=%fused_computation | loop fusion | bytes 256 | tf_op jit(solution)/shard_map/squeeze | solution.py:517
  44.9 0.7 %reshape.7 = f32[16,32]{1,0:T(8,128)} reshape(f32[512]{0:T(512)S(1)} %reduce.3) | data formatting | bytes 4096 | tf_op jit(solution)/shard_map/reshape | solution.py:517

commit v2 on v1

--- a/solution.py
+++ b/solution.py
@@ -21,8 +21,9 @@
 BF16 = jnp.bfloat16
 
 CHUNKS = 8
-WALK_BLOCK = 512
+WALK_BLOCK = 1024
 MAIN_BLOCK = 256
+UNROLL = 4
 
 
 def iota(shape, dim):
@@ -217,9 +218,6 @@
             return carry
 
         lax.fori_loop(0, chunk // WALK_BLOCK, one, 0)
-
-        if rounds:
-            start_round(0, c)
         return carry
 
     if rounds:
@@ -227,9 +225,6 @@
         @pl.when(bit(last) == 0)
         def _():
             recv[last] = jnp.zeros(recv.shape[1:], F32)
-
-    pl.semaphore_wait(barrier, n_tm - 1 + n_path - 1)
-    lax.fori_loop(0, CHUNKS, walk_chunk, 0)
 
     party = party_ref[...]
     expiry = mat_ref[...]
@@ -271,6 +266,26 @@
     bday = (first_date + (brow & (dates - 1)) + 1).astype(F32)
     bias_col[...] = (-0.5 * dt * LOG2E) * bvol * bvol * bday
     acc[...] = jnp.zeros_like(acc)
+
+    early = CHUNKS // 2
+    lax.fori_loop(0, early, walk_chunk, 0)
+    pl.semaphore_wait(barrier, n_tm - 1 + n_path - 1)
+
+    def send_early(c, carry):
+        start_round(0, c)
+        return carry
+
+    def walk_and_send(c, carry):
+        walk_chunk(c, carry)
+        start_round(0, c)
+        return carry
+
+    if rounds:
+        lax.fori_loop(0, early, send_early, 0)
+        lax.fori_loop(early, CHUNKS, walk_and_send, 0)
+    else:
+        lax.fori_loop(early, CHUNKS, walk_chunk, 0)
+
 
     def join(k, c):
         mine, theirs = pay[k - 1, c], recv[k - 1, c]
@@ -303,13 +318,13 @@
     carry_gain = jnp.exp(-lam * (iota((dates, 128), 0).astype(F32) + 1.0))
     ones = jnp.ones((3 * dates, MAIN_BLOCK), BF16)
 
-    def main_part(c, first):
+    def main_part(c, first, u):
         at = c * chunk + first
         cols = pl.ds(pl.multiple_of(at, MAIN_BLOCK), MAIN_BLOCK)
         own = pl.ds(pl.multiple_of(first, MAIN_BLOCK), MAIN_BLOCK)
         start = state[:, own]
         shifted = walk[:dates, cols] + wide(carry_gain, MAIN_BLOCK) * start[0:1] + RATE_SHIFT
-        inten[...] = (BASE_INTENSITY * dt) + (0.5 * dt) * (shifted * shifted)
+        inten[u] = (BASE_INTENSITY * dt) + (0.5 * dt) * (shifted * shifted)
         spots = []
         for j in range(nccy):
             log = walk[(j + 1) * dates : (j + 2) * dates, cols] + start[j + 1 : j + 2]
@@ -325,7 +340,7 @@
         hazard = start[quad_row : quad_row + 1]
         before = jnp.exp2(scales * hazard)
         for t in range(dates):
-            hazard = hazard + inten[t : t + 1, :]
+            hazard = hazard + inten[u, t : t + 1, :]
             after = jnp.exp2(scales * hazard)
             part = slice(t * ncp, (t + 1) * ncp)
             term = jnp.maximum(netted[part], 0.0) * (before - after)
@@ -353,10 +368,11 @@
         absorb(c)
 
         def one(b, carry):
-            main_part(c, b * MAIN_BLOCK)
+            for u in range(UNROLL):
+                main_part(c, (b * UNROLL + u) * MAIN_BLOCK, u)
             return carry
 
-        lax.fori_loop(0, chunk // MAIN_BLOCK, one, 0)
+        lax.fori_loop(0, chunk // (MAIN_BLOCK * UNROLL), one, 0)
         return carry
 
     lax.fori_loop(0, CHUNKS, main_chunk, 0)
@@ -390,7 +406,8 @@
     for i in range(1, n_path):
         total = total + row_recv[i]
     profile = total * (1.0 / (total_paths * dt))
-    profile_ref[...] = profile
+    for t in range(dates):
+        profile_ref[t : t + 1, :] = profile[:, t * ncp : (t + 1) * ncp]
 
     lane = iota((1, dates * ncp), 1)
     day = (first_date + lax.div(lane, ncp) + 1).astype(F32)
@@ -422,7 +439,7 @@
     cva = total
     for i in range(1, 128 // ncp):
         cva = cva + pltpu.roll(total, i * ncp, 1)
-    cva_ref[...] = cva
+    cva_ref[...] = cva[:, :ncp]
 
     def drain(c, carry):
         for k in range(rounds):
@@ -471,8 +488,8 @@
     profile, cva = pl.pallas_call(
         functools.partial(kernel, sizes),
         out_shape=(
-            jax.ShapeDtypeStruct((1, dates * ncp), F32),
-            jax.ShapeDtypeStruct((1, 128), F32),
+            jax.ShapeDtypeStruct((dates, ncp), F32),
+            jax.ShapeDtypeStruct((1, ncp), F32),
         ),
         in_specs=[smem] * 3 + [vmem] * 5 + [hbm] * 2,
         out_specs=(vmem, vmem),
@@ -485,7 +502,7 @@
             pltpu.VMEM((max(rounds, 1), CHUNKS, 8, chunk), F32),
             pltpu.VMEM((max(rounds, 1), CHUNKS, 8, chunk), F32),
             pltpu.VMEM((8, chunk), F32),
-            pltpu.VMEM((dates, MAIN_BLOCK), F32),
+            pltpu.VMEM((UNROLL, dates, MAIN_BLOCK), F32),
             pltpu.VMEM((dates * ncp, 128), F32),
             pltpu.VMEM((ncp, 128), F32),
             pltpu.VMEM((nccy * dates, 128), F32),
@@ -514,7 +531,7 @@
         shock_rate,
         shock_fx,
     )
-    return (profile.reshape(dates, ncp), cva[0, :ncp])
+    return (profile, cva.reshape(ncp))
 
 
 def solution(mesh):

time: 45.7 us -> 37 us (0.81)
  Pallas kernels: 41.3 us -> 33.7 us
  other arithmetic: 1.34 us -> 0 us
    pallas_call x1, Pallas kernels: 41.3 us -> 33.7 us  [per_device(): pl.pallas_call(functools.partial(kernel, sizes), out_shape=(jax.ShapeDtyp...]
    unnamed x0 -> x2, local copies, waits for them, and re-layouts: none -> 2.43 us
    pallas_call x1 -> x0, other arithmetic: 1.34 us -> none  [per_device(): pl.pallas_call(functools.partial(kernel, sizes), out_shape=(jax.ShapeDtyp...]
    squeeze x1 -> x0, local copies, waits for them, and re-layouts: 1.11 us -> none  [per_device(): return (profile.reshape(dates, ncp), cva[0, :ncp])]
    reshape x1 -> x0, local copies, waits for them, and re-layouts: 0.67 us -> none  [per_device(): return (profile.reshape(dates, ncp), cva[0, :ncp])]
    pallas_call x1 -> x0, local copies, waits for them, and re-layouts: 0.51 us -> none  [per_device(): pl.pallas_call(functools.partial(kernel, sizes), out_shape=(jax.ShapeDtyp...]
where the time goes in v2:
time: 37 us; the launch traced here: 36.7 us
  Pallas kernels  33.7 us (91%)
  local copies, waits for them, and re-layouts  2.43 us (7%)
  between operations  0.64 us (2%)
    pallas_call x1, Pallas kernels, per_device(): pl.pallas_call(functools.partial(kernel, sizes), out_shape=(jax.ShapeDtyp...  33.7 us
    unnamed x2, local copies, waits for them, and re-layouts  2.43 us

profile of v2, /device:TPU:0, one launch (start us, length us, event | category | flops | bytes accessed | tf_op | source)
XLA Modules:
  0.0 36.7 jit_solution(3242228775032736905)
XLA Ops:
  0.6 33.7 %shard_map.113 = (f32[16,32]{1,0:T(8,128)}, f32[1,32]{1,0:T(1,128)}) custom-call(f32[4]{0:T(128)} %vol_ref.1, f32[4]{0:T(128)} %corr_ref.1, f32[32]{0:T(128)} %scale_ref.1, s32[1,512]{1,0:T(1,128)} %bitcast.6, s32[1,512]{1,0:T(1,128)} %bitcast.7, s32[1,512]{1,0:T(1,128)} %bitcast.8, f32[1,512]{1,0:T(1,128)} %bitcast.9, f32[1,512]{1,0:T(1,128)} %bitcast.10, ...), custom_call_target="tpu_custom_call" | custom-call | tf_op jit(solution)/shard_map/pallas_call | solution.py:488
  34.3 1.3 %copy.14 = f32[16,32]{1,0:T(8,128)} copy(f32[16,32]{1,0:T(8,128)} %get-tuple-element.8) | data formatting | bytes 4096
  35.6 1.1 %copy.15 = f32[32]{0:T(128)} copy(f32[32]{0:T(128)} %bitcast.11) | data formatting | bytes 256
